TPU v7x, 32 devices: a whole 2x2x4 slice. The times are simulated.
32 devices in a mesh: tm: 8 (over z, x), tile: 4 (over y, core).
Axes of the slice: x: 2, y: 2, z: 4, core: 2. Of those that a mesh axis runs over, the one named last changes fastest.
Arguments:
- returns: float32 [2048, 2048], P('tm', 'tile'), may hold values from -6 to 6
- decay_rates: float32 [2048], replicated, may hold values from 9.765625e-05 to 0.015625, as said below
Outputs:
- covariance: float32 [8, 2048, 2048], P('tm', 'tile')
Inputs may be any that keep to these rules, and one draw needn't show every extreme that they name: `decay_rates`: every rate is positive.
All inputs are finite; a program needn't handle non-finite values.
Results may differ from a plain program's by a relative error of at most 0.0039.
Values may be sent and summed in bfloat16 or wider, within the bound.
A program may use at most 128 MiB of HBM per device.

v0:
```python
import jax
import jax.numpy as jnp
from jax import lax
from jax.sharding import PartitionSpec as P


def per_device(returns, decay_rates):
    seg_days, col_block = returns.shape
    tile_at = lax.axis_index("tile")
    seg_at = lax.axis_index("tm")
    days_left = (seg_days - 1 - jnp.arange(seg_days)).astype(jnp.float32)
    own_rates = lax.dynamic_slice_in_dim(decay_rates, tile_at * col_block, col_block)
    scaled = (returns * jnp.exp(-own_rates[None, :] * days_left[:, None])).astype(jnp.bfloat16)
    gram_rows = lax.dot_general(
        scaled,
        lax.all_gather(scaled, "tile", axis=1, tiled=True),
        (((0,), (0,)), ((), ())),
        preferred_element_type=jnp.float32,
    )
    pair_rate = own_rates[:, None] + decay_rates[None, :]
    seg_decay = jnp.exp(-pair_rate * seg_days)
    periods = lax.axis_size("tm")
    row_piece = col_block // periods
    spread = lax.all_to_all(gram_rows[None], "tm", split_axis=1, concat_axis=0, tiled=True)
    row_rates = lax.dynamic_slice_in_dim(
        decay_rates, tile_at * col_block + seg_at * row_piece, row_piece
    )
    row_decay = jnp.exp(-(row_rates[:, None] + decay_rates[None, :]) * seg_days)

    def advance(running, segment_term):
        return (running * row_decay + segment_term, running)

    _, prefix = lax.scan(advance, jnp.zeros_like(spread[0]), spread)
    carried = lax.all_to_all(prefix, "tm", split_axis=0, concat_axis=1, tiled=True)[0]
    running = carried * seg_decay + gram_rows
    elapsed = (seg_at + 1).astype(jnp.float32) * seg_days
    weights = jnp.expm1(-pair_rate * elapsed) / jnp.expm1(-pair_rate)
    return (running / weights)[None]


def solution(mesh):
    placed = (P("tm", "tile"), P())
    return jax.shard_map(
        per_device, mesh=mesh, in_specs=placed, out_specs=P("tm", "tile", None), check_vma=False
    )
```

profile of v0, /device:TPU:27, one launch (start us, length us, event | category | flops | bytes accessed | tf_op | source)
XLA Modules:
  0.0 272.1 jit_solution(13295969740245957203)
XLA Ops:
  6.5 0.0 all-gather.2.cloned.1.call-start
  6.5 0.8 fusion.5
  7.3 1.9 multiply_convert_fusion
  9.2 0.0 all-gather.2.cloned.1.call-update
  9.2 18.2 %all-gather.2.cloned.1.call-done = bf16[256,2048]{1,0:T(8,128)(2,1)} async-done(((bf16[256,512]{1,0:T(8,128)(2,1)}), bf16[256,2048]{1,0:T(8,128)(2,1)}) %all-gather.2.cloned.1.call-update) | async-done | bytes 1048592 | tf_op jit(solution)/shard_map/all_gather | solution.py:16
  27.4 2.0 fusion.6
  29.5 0.0 copy-start
  29.5 2.0 copy-done
  31.5 6.3 %copy.3 = f32[1,512,2048]{2,0,1:T(1,128)} copy(f32[1,512,2048]{2,1,0:T(8,128)S(1)} %bitcast.21) | data formatting | bytes 8388608 | tf_op jit(solution)/shard_map/broadcast_in_dim | solution.py:24
  37.7 0.0 copy-start.1
  37.7 5.6 %all-to-all-start = ((f32[1,512,2048]{2,0,1:T(1,128)}), f32[1,512,2048]{2,0,1:T(1,128)}, u32[]{:S(2)}, u32[]{:S(2)}) async-start(f32[1,512,2048]{2,0,1:T(1,128)} %copy.3), calls=%async_computation | async-start | bytes 8388608 | tf_op jit(solution)/shard_map/all_to_all | solution.py:24
  43.3 0.0 copy-done.1
  43.3 0.1 dynamic_slice.10
  43.4 91.6 %all-to-all-done = f32[1,512,2048]{2,0,1:T(1,128)} async-done(((f32[1,512,2048]{2,0,1:T(1,128)}), f32[1,512,2048]{2,0,1:T(1,128)}, u32[]{:S(2)}, u32[]{:S(2)}) %all-to-all-start) | async-done | bytes 4194336 | tf_op jit(solution)/shard_map/all_to_all | solution.py:24
  135.0 6.1 %copy.4 = f32[1,512,2048]{2,1,0:T(8,128)} copy(f32[1,512,2048]{2,0,1:T(1,128)} %all-to-all-done) | data formatting | bytes 8388608
  141.1 17.5 %while.13 = (s32[]{:T(128)}, f32[64,2048]{1,0:T(8,128)S(1)}, f32[8,64,2048]{2,1,0:T(8,128)}, f32[8,64,2048]{2,1,0:T(8,128)}, f32[2048]{0:T(1024)S(1)}, /*index=5*/f32[64]{0:T(128)S(1)}, s32[]{:T(128)}, s32[]{:T(128)}) while((s32[]{:T(128)}, f32[64,2048]{1,0:T(8,128)S(1)}, f32[8,64,2048]{2,1,0:T(8,128)}, f32[8,64,2048]{2,1,0:T(8,128)}, ...), condition=%wide.region_1.2_spmd.clone, body=%wide.region_0.1_spmd.clone.sunk | while | flops 917507 | bytes 2630000 | solution.py:33
  141.1 0.8 bitcast_dynamic-update-slice_fusion.2
  141.9 1.3 bitcast_add_fusion.2
  143.3 0.8 bitcast_dynamic-update-slice_fusion.2
  144.1 1.3 bitcast_add_fusion.2
  145.4 0.9 bitcast_dynamic-update-slice_fusion.2
  146.3 1.3 bitcast_add_fusion.2
  147.6 0.8 bitcast_dynamic-update-slice_fusion.2
  148.5 1.3 bitcast_add_fusion.2
  149.8 0.9 bitcast_dynamic-update-slice_fusion.2
  150.7 1.3 bitcast_add_fusion.2
  152.0 0.8 bitcast_dynamic-update-slice_fusion.2
  152.8 1.3 bitcast_add_fusion.2
  154.2 0.8 bitcast_dynamic-update-slice_fusion.2
  155.0 1.3 bitcast_add_fusion.2
  156.4 0.9 bitcast_dynamic-update-slice_fusion.2
  157.3 1.3 bitcast_add_fusion.2
  158.6 5.7 %all-to-all-start.1 = ((f32[8,64,2048]{2,1,0:T(8,128)}), f32[8,64,2048]{2,1,0:T(8,128)}, u32[]{:S(2)}, u32[]{:S(2)}) async-start(f32[8,64,2048]{2,1,0:T(8,128)} %get-tuple-element.32), calls=%async_computation.1 | async-start | bytes 8388608 | tf_op jit(solution)/shard_map/all_to_all | solution.py:34
  164.3 91.6 %all-to-all-done.1 = f32[8,64,2048]{2,1,0:T(8,128)} async-done(((f32[8,64,2048]{2,1,0:T(8,128)}), f32[8,64,2048]{2,1,0:T(8,128)}, u32[]{:S(2)}, u32[]{:S(2)}) %all-to-all-start.1) | async-done | bytes 4194336 | tf_op jit(solution)/shard_map/all_to_all | solution.py:34
  255.9 9.3 %fusion.4 = f32[512,2048]{1,0:T(8,128)} fusion(f32[512,2048]{1,0:T(8,128)} %copy-done, f32[8,64,2048]{2,1,0:T(8,128)} %all-to-all-done.1, f32[]{:T(128)S(6)} %mul.61, f32[2048]{0:T(1024)S(1)} %get-tuple-element.141, f32[512]{0:T(512)S(1)} %get-tuple-element.71), kind=kLoop, calls=%fused_computation.7 | loop fusion | flops 8388608 | bytes 12593156 | tf_op jit(solution)/shard_map/div | solution.py:38
  (3 shorter events, 0.0 us)
Async XLA Ops:
  6.5 20.9 %all-gather.2.cloned.1.call-start = ((), (), s32[]{:S(2)}) async-start(), calls=%async_computation.2 | async-start | bytes 1310720 | tf_op jit(solution)/shard_map/all_gather | solution.py:16
  29.5 2.0 copy-start
  37.7 5.6 %copy-start.1 = (f32[2048]{0:T(1024)S(1)}, f32[2048]{0:T(1024)}, u32[]{:S(2)}) copy-start(f32[2048]{0:T(1024)} %param.5) | copy-start | bytes 24580
  37.7 97.2 %all-to-all-start = ((f32[1,512,2048]{2,0,1:T(1,128)}), f32[1,512,2048]{2,0,1:T(1,128)}, u32[]{:S(2)}, u32[]{:S(2)}) async-start(f32[1,512,2048]{2,0,1:T(1,128)} %copy.3), calls=%async_computation | async-start | bytes 8388608 | tf_op jit(solution)/shard_map/all_to_all | solution.py:24
  158.6 97.3 %all-to-all-start.1 = ((f32[8,64,2048]{2,1,0:T(8,128)}), f32[8,64,2048]{2,1,0:T(8,128)}, u32[]{:S(2)}, u32[]{:S(2)}) async-start(f32[8,64,2048]{2,1,0:T(8,128)} %get-tuple-element.32), calls=%async_computation.1 | async-start | bytes 8388608 | tf_op jit(solution)/shard_map/all_to_all | solution.py:34
Sparse Core Ops, SparseCore 0:
  9.3 18.0 all-gather.1
where the time goes:
time: 276 us; the launch traced here: 272 us
  waiting for transfers between devices  201 us (73%)
  other arithmetic  29.3 us (11%)
  local copies, waits for them, and re-layouts  14.4 us (5%)
  between operations  13.4 us (5%)
  starting transfers between devices  11.2 us (4%)
    all_to_all x1, waiting for transfers between devices, per_device(): lax.all_to_all(prefix, 'tm', split_axis=0, concat_axis=1, tiled=True)[0]  91.6 us
    all_to_all x1, waiting for transfers between devices, per_device(): lax.all_to_all(gram_rows[None], 'tm', split_axis=1, concat_axis=0, tiled=...  91.6 us
    all_gather x1, waiting for transfers between devices, per_device(): lax.all_gather(scaled, 'tile', axis=1, tiled=True)  18.2 us
    add x8, other arithmetic, advance(): return (running * row_decay + segment_term, running)  10.5 us
    div x1, other arithmetic, per_device(): return (running / weights)[None]  9.33 us
    unnamed x5, local copies, waits for them, and re-layouts  8.1 us
    dynamic_update_slice x8, other arithmetic, per_device(): _, prefix = lax.scan(advance, jnp.zeros_like(spread[0]), spread)  6.83 us
    broadcast_in_dim x1, local copies, waits for them, and re-layouts, per_device(): gram_rows[None]  6.26 us
  transfers between devices with their start and end apart: 3, of which 3 were waited for; matrix products, arithmetic and copies ran while one was open for 0% of the time, Pallas kernels for 0%

commit v1 on v0

--- a/solution.py
+++ b/solution.py
@@ -1,10 +1,206 @@
+import functools
+
 import jax
 import jax.numpy as jnp
 from jax import lax
+from jax.experimental import pallas as pl
+from jax.experimental.pallas import tpu as pltpu
 from jax.sharding import PartitionSpec as P
 
-
-def per_device(returns, decay_rates):
+MESH = pl.DeviceIdType.MESH
+F32 = jnp.float32
+CORES = 2
+
+
+def expm1_neg(x):
+    near = jnp.maximum(x, -0.5)
+    series = jnp.ones_like(x)
+    for n in range(9, 1, -1):
+        series = 1.0 + near * (1.0 / n) * series
+    return jnp.where(x > -0.5, near * series, jnp.exp(x) - 1.0)
+
+
+def gather_kernel(periods, tiles, returns_ref, rates_ref, out_ref, buf, cols, ssem, rsem):
+    seg_days, block = returns_ref.shape
+    width = tiles // CORES
+    planes = periods // width
+    half = seg_days // 2
+    s = lax.axis_index("tm")
+    t = lax.axis_index("tile")
+    z, x = s // width, s % width
+    y, c = t // CORES, t % CORES
+    yt = (1 - y) * CORES + c
+    pt = y * CORES + (1 - c)
+    pyt = (1 - y) * CORES + (1 - c)
+    sx = z * width + (1 - x)
+    x_dev, y_dev, p_dev = (sx, t), (s, yt), (s, pt)
+    up_dev, down_dev = (s + width, t), (s - width, t)
+    has_up, has_down = z < planes - 1, z > 0
+
+    barrier = pltpu.get_barrier_semaphore()
+    for dev in (x_dev, y_dev, p_dev):
+        pl.semaphore_signal(barrier, inc=1, device_id=dev, device_id_type=MESH)
+
+    @pl.when(has_up)
+    def _():
+        pl.semaphore_signal(barrier, inc=1, device_id=up_dev, device_id_type=MESH)
+
+    @pl.when(has_down)
+    def _():
+        pl.semaphore_signal(barrier, inc=1, device_id=down_dev, device_id_type=MESH)
+
+    own = pl.ds(pl.multiple_of(t * block, block), block)
+    own_rates = rates_ref[:, own]
+    days_left = (seg_days - 1 - lax.broadcasted_iota(jnp.int32, (seg_days, block), 0)).astype(F32)
+    buf[s, t] = (returns_ref[...] * jnp.exp(-own_rates * days_left)).astype(jnp.bfloat16)
+    cols[...] = jnp.transpose(jnp.broadcast_to(own_rates, (128, block)))
+
+    pl.semaphore_wait(barrier, 3 + has_up.astype(jnp.int32) + has_down.astype(jnp.int32))
+
+    sent = []
+
+    def copy(sp, tp, h, dev, sem):
+        part = buf.at[sp, tp, pl.ds(h * half, half)]
+        return pltpu.make_async_remote_copy(
+            part, part, sem, rsem.at[sp, tp, h], device_id=dev, device_id_type=MESH
+        )
+
+    def arrived(sp, tp, h):
+        copy(sp, tp, h, p_dev, ssem.at[0, 0]).wait_recv()
+
+    def plane(d):
+        exists = z >= d
+        sa = (z - d) * width + x
+        sb = (z - d) * width + (1 - x)
+        x_takes = exists & (sa <= sx)
+        x_gives = exists & (sb <= s)
+        count = [0]
+
+        def send(cond, sp, tp, h, dev):
+            sem = ssem.at[d, count[0]]
+            count[0] += 1
+            sent.append((cond, sp, tp, h, dev, sem))
+
+            @pl.when(cond)
+            def _():
+                copy(sp, tp, h, dev, sem).start()
+
+        def wait(cond, sp, tp, h):
+            @pl.when(cond)
+            def _():
+                arrived(sp, tp, h)
+
+        def column():
+            for h in (0, 1):
+                if d:
+                    wait(exists, sa, t, h)
+                send(exists & has_up, sa, t, h, up_dev)
+                send(x_takes, sa, t, h, x_dev)
+                send(exists, sa, t, h, y_dev)
+                send(exists, sa, t, h, p_dev)
+
+        def across():
+            for h in (0, 1):
+                wait(x_gives, sb, t, h)
+                if h == 0:
+                    send(x_gives, sb, t, h, y_dev)
+                send(x_gives, sb, t, h, p_dev)
+                wait(exists, sa, yt, h)
+                if h == 1:
+                    send(x_takes, sa, yt, h, x_dev)
+                send(exists, sa, yt, h, p_dev)
+            for h in (0, 1):
+                wait(x_gives, sb, yt, h)
+                send(x_gives, sb, yt, h, p_dev)
+
+        def partner():
+            for h in (0, 1):
+                wait(exists, sa, pt, h)
+                wait(exists, sa, pyt, h)
+                wait(x_gives, sb, pt, h)
+                wait(x_gives, sb, pyt, h)
+
+        def compute():
+            for cond, sp in ((exists, sa), (x_gives, sb)):
+
+                @pl.when(cond)
+                def _(sp=sp):
+                    lag = ((s - sp) * seg_days).astype(F32)
+                    lhs = buf[sp, t]
+                    col = jnp.exp(-cols[...] * lag)
+
+                    def step(tp, _):
+                        at = pl.ds(pl.multiple_of(tp * block, block), block)
+                        gram = lax.dot_general(
+                            lhs, buf[sp, tp], (((0,), (0,)), ((), ())), preferred_element_type=F32
+                        )
+                        row = jnp.exp(-rates_ref[:, at] * lag)
+                        for j in range(block // 128):
+                            lane = slice(j * 128, (j + 1) * 128)
+                            here = pl.ds(pl.multiple_of(tp * block + j * 128, 128), 128)
+                            term = gram[:, lane] * (col * row[:, lane])
+                            if d == 0 and sp is sa:
+                                out_ref[:, here] = term
+                            else:
+                                out_ref[:, here] += term
+                        return 0
+
+                    lax.fori_loop(0, tiles, step, 0)
+
+        return column, across, partner, compute
+
+    steps = [plane(d) for d in range(planes)]
+    steps[0][0]()
+    for d in range(planes):
+        if d + 1 < planes:
+            steps[d + 1][0]()
+        for stage in steps[d][1:]:
+            stage()
+
+    elapsed = ((s + 1) * seg_days).astype(F32)
+    u1, un = expm1_neg(-cols[...]), expm1_neg(-cols[...] * elapsed)
+
+    def finish(j, _):
+        at = pl.ds(pl.multiple_of(j * 128, 128), 128)
+        rates = rates_ref[:, at]
+        v1, vn = expm1_neg(-rates), expm1_neg(-rates * elapsed)
+        out_ref[:, at] = out_ref[:, at] * ((u1 + v1 + u1 * v1) / (un + vn + un * vn))
+        return 0
+
+    lax.fori_loop(0, out_ref.shape[1] // 128, finish, 0)
+
+    for cond, sp, tp, h, dev, sem in sent:
+
+        @pl.when(cond)
+        def _(sp=sp, tp=tp, h=h, dev=dev, sem=sem):
+            copy(sp, tp, h, dev, sem).wait_send()
+
+
+def by_gather(returns, decay_rates):
+    seg_days, block = returns.shape
+    periods, tiles = lax.axis_size("tm"), lax.axis_size("tile")
+    assets = decay_rates.shape[0]
+    planes = periods // (tiles // CORES)
+    vmem = pl.BlockSpec(memory_space=pltpu.VMEM)
+    return pl.pallas_call(
+        functools.partial(gather_kernel, periods, tiles),
+        out_shape=jax.ShapeDtypeStruct((block, assets), F32),
+        in_specs=[vmem, vmem],
+        out_specs=vmem,
+        scratch_shapes=[
+            pltpu.VMEM((periods, tiles, seg_days, block), jnp.bfloat16),
+            pltpu.VMEM((block, 128), F32),
+            pltpu.SemaphoreType.DMA((planes, 18)),
+            pltpu.SemaphoreType.DMA((periods, tiles, 2)),
+        ],
+        compiler_params=pltpu.CompilerParams(
+            collective_id=0, has_side_effects=True, vmem_limit_bytes=40 * 2**20
+        ),
+        name="gather_sums",
+    )(returns, decay_rates[None])[None]
+
+
+def by_exchange(returns, decay_rates):
     seg_days, col_block = returns.shape
     tile_at = lax.axis_index("tile")
     seg_at = lax.axis_index("tm")
@@ -40,6 +236,8 @@
 
 def solution(mesh):
     placed = (P("tm", "tile"), P())
+    pairs = mesh.shape["tile"] == 2 * CORES
+    per_device = by_gather if pairs else by_exchange
     return jax.shard_map(
         per_device, mesh=mesh, in_specs=placed, out_specs=P("tm", "tile", None), check_vma=False
     )

time: 276 us -> 72.5 us (0.26); the launches traced: 272 us -> 72.3 us
  waiting for transfers between devices: 201 us -> 0 us
  Pallas kernels: 0 us -> 68.6 us
  other arithmetic: 29.3 us -> 0 us
  between operations: 13.4 us -> 0.01 us
  starting transfers between devices: 11.2 us -> 0 us
  local copies, waits for them, and re-layouts: 14.4 us -> 3.75 us
    all_to_all x2 -> x0, waiting for transfers between devices: 183 us -> none  [the longest x1 91.6 us: per_device(): lax.all_to_all(prefix, 'tm', split_axis=0, concat_axis=1, tiled=True)[0]]
    pallas_call x0 -> x1, Pallas kernels: none -> 68.6 us  [by_gather(): pl.pallas_call(functools.partial(gather_kernel, periods, tiles), out_shap...]
    all_gather x1 -> x0, waiting for transfers between devices: 18.2 us -> none  [per_device(): lax.all_gather(scaled, 'tile', axis=1, tiled=True)]
    all_to_all x2 -> x0, starting transfers between devices: 11.2 us -> none  [the longest x1 5.67 us: per_device(): lax.all_to_all(prefix, 'tm', split_axis=0, concat_axis=1, tiled=True)[0]]
    add x8 -> x0, other arithmetic: 10.5 us -> none  [advance(): return (running * row_decay + segment_term, running)]
    div x1 -> x0, other arithmetic: 9.33 us -> none  [per_device(): return (running / weights)[None]]
    dynamic_update_slice x8 -> x0, other arithmetic: 6.83 us -> none  [per_device(): _, prefix = lax.scan(advance, jnp.zeros_like(spread[0]), spread)]
    broadcast_in_dim x1 -> x0, local copies, waits for them, and re-layouts: 6.26 us -> none  [per_device(): gram_rows[None]]
  transfers between devices with their start and end apart: 3 -> 0, of which waited for: 3 -> 0; matrix products, arithmetic and copies ran while one was open for 0% -> 0% of each run, Pallas kernels for 0% -> 0%
where the time goes in v1:
time: 72.5 us; the launch traced here: 72.3 us
  Pallas kernels  68.6 us (95%)
  local copies, waits for them, and re-layouts  3.75 us (5%)
    pallas_call x1, Pallas kernels, by_gather(): pl.pallas_call(functools.partial(gather_kernel, periods, tiles), out_shap...  68.6 us
    unnamed x5, local copies, waits for them, and re-layouts  3.75 us

profile of v1, /device:TPU:27, one launch (start us, length us, event | category | flops | bytes accessed | tf_op | source)
XLA Modules:
  0.0 72.3 jit_solution(7483023159056841169)
XLA Ops:
  0.0 0.0 copy-start
  0.0 1.0 %copy-done = f32[256,512]{1,0:T(8,128)S(1)} copy-done((f32[256,512]{1,0:T(8,128)S(1)}, f32[256,512]{1,0:T(8,128)}, u32[]{:S(2)}) %copy-start) | copy-done | bytes 524312
  1.0 0.0 copy-start.1
  1.0 0.7 copy-done.1
  1.7 68.6 %gather_sums.1 = f32[512,2048]{1,0:T(8,128)S(1)} custom-call(f32[256,512]{1,0:T(8,128)S(1)} %copy-done, f32[1,2048]{1,0:T(1,128)S(1)} %bitcast.3), custom_call_target="tpu_custom_call" | custom-call | tf_op jit(solution)/shard_map/gather_sums/pallas_call | solution.py:185
  70.3 2.0 %copy.4 = f32[1,512,2048]{2,1,0:T(8,128)} copy(f32[1,512,2048]{2,1,0:T(8,128)S(1)} %bitcast.2) | data formatting | bytes 8388608
Async XLA Ops:
  0.0 1.0 %copy-start = (f32[256,512]{1,0:T(8,128)S(1)}, f32[256,512]{1,0:T(8,128)}, u32[]{:S(2)}) copy-start(f32[256,512]{1,0:T(8,128)} %returns_ref.1) | copy-start | bytes 1572868
  1.0 0.7 copy-start.1

commit v2 on v1

--- a/solution.py
+++ b/solution.py
@@ -20,7 +20,9 @@
     return jnp.where(x > -0.5, near * series, jnp.exp(x) - 1.0)
 
 
-def gather_kernel(periods, tiles, returns_ref, rates_ref, out_ref, buf, cols, ssem, rsem):
+def gather_kernel(
+    periods, tiles, returns_ref, rates_ref, out_ref, buf, left, cols, ssem, rsem
+):
     seg_days, block = returns_ref.shape
     width = tiles // CORES
     planes = periods // width
@@ -49,6 +51,7 @@
     def _():
         pl.semaphore_signal(barrier, inc=1, device_id=down_dev, device_id_type=MESH)
 
+    out_ref[...] = jnp.zeros_like(out_ref)
     own = pl.ds(pl.multiple_of(t * block, block), block)
     own_rates = rates_ref[:, own]
     days_left = (seg_days - 1 - lax.broadcasted_iota(jnp.int32, (seg_days, block), 0)).astype(F32)
@@ -90,84 +93,126 @@
             def _():
                 arrived(sp, tp, h)
 
-        def column():
-            for h in (0, 1):
-                if d:
-                    wait(exists, sa, t, h)
-                send(exists & has_up, sa, t, h, up_dev)
-                send(x_takes, sa, t, h, x_dev)
-                send(exists, sa, t, h, y_dev)
-                send(exists, sa, t, h, p_dev)
-
-        def across():
-            for h in (0, 1):
-                wait(x_gives, sb, t, h)
-                if h == 0:
-                    send(x_gives, sb, t, h, y_dev)
-                send(x_gives, sb, t, h, p_dev)
-                wait(exists, sa, yt, h)
-                if h == 1:
-                    send(x_takes, sa, yt, h, x_dev)
-                send(exists, sa, yt, h, p_dev)
+        def column(h):
+            if d:
+                wait(exists, sa, t, h)
+            send(exists & has_up, sa, t, h, up_dev)
+            send(x_takes, sa, t, h, x_dev)
+            send(exists, sa, t, h, y_dev)
+            send(exists, sa, t, h, p_dev)
+
+        def across(h):
+            wait(x_gives, sb, t, h)
+            if h == 0:
+                send(x_gives, sb, t, h, y_dev)
+            send(x_gives, sb, t, h, p_dev)
+            wait(exists, sa, yt, h)
+            if h == 1:
+                send(x_takes, sa, yt, h, x_dev)
+            send(exists, sa, yt, h, p_dev)
+
+        def corner():
             for h in (0, 1):
                 wait(x_gives, sb, yt, h)
                 send(x_gives, sb, yt, h, p_dev)
 
-        def partner():
+        def transpose(sp):
+            left[sp] = jnp.transpose(buf[sp, t])
+
+        def product(sp, tp):
+            lag = ((s - sp) * seg_days).astype(F32)
+            gram = jnp.dot(left[sp], buf[sp, tp], preferred_element_type=F32)
+            at = pl.ds(pl.multiple_of(tp * block, block), block)
+            col, row = jnp.exp(-cols[...] * lag), jnp.exp(-rates_ref[:, at] * lag)
+            for j in range(block // 128):
+                lane = slice(j * 128, (j + 1) * 128)
+                here = pl.ds(pl.multiple_of(tp * block + j * 128, 128), 128)
+                out_ref[:, here] += gram[:, lane] * (col * row[:, lane])
+
+        def products(first, last, which):
+            def step(i, _):
+                product(*which(i))
+                return 0
+
+            lax.fori_loop(first, last, step, 0)
+
+        def column_products():
+            @pl.when(exists)
+            def _():
+                for h in (0, 1):
+                    arrived(sa, pt, h)
+                transpose(sa)
+                products(0, 2, lambda i: (sa, y * CORES + i))
+
+        def across_products():
             for h in (0, 1):
-                wait(exists, sa, pt, h)
+                wait(x_gives, sb, pt, h)
                 wait(exists, sa, pyt, h)
-                wait(x_gives, sb, pt, h)
-                wait(x_gives, sb, pyt, h)
-
-        def compute():
-            for cond, sp in ((exists, sa), (x_gives, sb)):
-
-                @pl.when(cond)
-                def _(sp=sp):
-                    lag = ((s - sp) * seg_days).astype(F32)
-                    lhs = buf[sp, t]
-                    col = jnp.exp(-cols[...] * lag)
-
-                    def step(tp, _):
-                        at = pl.ds(pl.multiple_of(tp * block, block), block)
-                        gram = lax.dot_general(
-                            lhs, buf[sp, tp], (((0,), (0,)), ((), ())), preferred_element_type=F32
-                        )
-                        row = jnp.exp(-rates_ref[:, at] * lag)
-                        for j in range(block // 128):
-                            lane = slice(j * 128, (j + 1) * 128)
-                            here = pl.ds(pl.multiple_of(tp * block + j * 128, 128), 128)
-                            term = gram[:, lane] * (col * row[:, lane])
-                            if d == 0 and sp is sa:
-                                out_ref[:, here] = term
-                            else:
-                                out_ref[:, here] += term
-                        return 0
-
-                    lax.fori_loop(0, tiles, step, 0)
-
-        return column, across, partner, compute
-
-    steps = [plane(d) for d in range(planes)]
-    steps[0][0]()
+
+            @pl.when(x_gives)
+            def _():
+                transpose(sb)
+
+            @pl.when(exists)
+            def _():
+                products(
+                    jnp.where(x_gives, 0, 2),
+                    4,
+                    lambda i: (
+                        jnp.where(i < 2, sb, sa),
+                        jnp.where(i < 2, y * CORES + i, (1 - y) * CORES + i - 2),
+                    ),
+                )
+
+        def corner_products():
+            @pl.when(x_gives)
+            def _():
+                for h in (0, 1):
+                    arrived(sb, pyt, h)
+                products(0, 2, lambda i: (sb, (1 - y) * CORES + i))
+
+        return column, across, corner, column_products, across_products, corner_products
+
+    column, across, corner, column_products, across_products, corner_products = zip(
+        *[plane(d) for d in range(planes)]
+    )
+
+    elapsed = ((s + 1) * seg_days).astype(F32)
+
+    def finish(first):
+        u1, un = expm1_neg(-cols[...]), expm1_neg(-cols[...] * elapsed)
+
+        def step(j, _):
+            at = pl.ds(pl.multiple_of(first * block + j * 128, 128), 128)
+            rates = rates_ref[:, at]
+            v1, vn = expm1_neg(-rates), expm1_neg(-rates * elapsed)
+            out_ref[:, at] = out_ref[:, at] * ((u1 + v1 + u1 * v1) / (un + vn + un * vn))
+            return 0
+
+        lax.fori_loop(0, CORES * block // 128, step, 0)
+
+    column[0](0)
+    column[0](1)
+    column_products[0]()
     for d in range(planes):
-        if d + 1 < planes:
-            steps[d + 1][0]()
-        for stage in steps[d][1:]:
-            stage()
-
-    elapsed = ((s + 1) * seg_days).astype(F32)
-    u1, un = expm1_neg(-cols[...]), expm1_neg(-cols[...] * elapsed)
-
-    def finish(j, _):
-        at = pl.ds(pl.multiple_of(j * 128, 128), 128)
-        rates = rates_ref[:, at]
-        v1, vn = expm1_neg(-rates), expm1_neg(-rates * elapsed)
-        out_ref[:, at] = out_ref[:, at] * ((u1 + v1 + u1 * v1) / (un + vn + un * vn))
-        return 0
-
-    lax.fori_loop(0, out_ref.shape[1] // 128, finish, 0)
+        more = d + 1 < planes
+        if more:
+            column[d + 1](0)
+        if d:
+            corner[d - 1]()
+        across[d](0)
+        if more:
+            column[d + 1](1)
+        across[d](1)
+        if d:
+            corner_products[d - 1]()
+        across_products[d]()
+        if more:
+            column_products[d + 1]()
+    finish(y * CORES)
+    corner[-1]()
+    corner_products[-1]()
+    finish((1 - y) * CORES)
 
     for cond, sp, tp, h, dev, sem in sent:
 
@@ -189,6 +234,7 @@
         out_specs=vmem,
         scratch_shapes=[
             pltpu.VMEM((periods, tiles, seg_days, block), jnp.bfloat16),
+            pltpu.VMEM((periods, block, seg_days), jnp.bfloat16),
             pltpu.VMEM((block, 128), F32),
             pltpu.SemaphoreType.DMA((planes, 18)),
             pltpu.SemaphoreType.DMA((periods, tiles, 2)),

time: 72.5 us -> 48.5 us (0.67)
  Pallas kernels: 68.6 us -> 44.1 us
    pallas_call x1, Pallas kernels: 68.6 us -> 44.1 us  [by_gather(): pl.pallas_call(functools.partial(gather_kernel, periods, tiles), out_shap...]
where the time goes in v2:
time: 48.5 us; the launch traced here: 47.9 us
  Pallas kernels  44.1 us (91%)
  local copies, waits for them, and re-layouts  3.75 us (8%)
    pallas_call x1, Pallas kernels, by_gather(): pl.pallas_call(functools.partial(gather_kernel, periods, tiles), out_shap...  44.1 us
    unnamed x5, local copies, waits for them, and re-layouts  3.75 us

profile of v2, /device:TPU:27, one launch (start us, length us, event | category | flops | bytes accessed | tf_op | source)
XLA Modules:
  0.0 47.9 jit_solution(10948029000522193641)
XLA Ops:
  0.0 0.0 copy-start
  0.0 1.0 %copy-done = f32[256,512]{1,0:T(8,128)S(1)} copy-done((f32[256,512]{1,0:T(8,128)S(1)}, f32[256,512]{1,0:T(8,128)}, u32[]{:S(2)}) %copy-start) | copy-done | bytes 524312
  1.0 0.0 copy-start.1
  1.0 0.7 %copy-done.1 = f32[2048]{0:T(1024)S(1)} copy-done((f32[2048]{0:T(1024)S(1)}, f32[2048]{0:T(1024)}, u32[]{:S(2)}) %copy-start.1) | copy-done | bytes 8216
  1.7 44.1 %gather_sums.1 = f32[512,2048]{1,0:T(8,128)S(1)} custom-call(f32[256,512]{1,0:T(8,128)S(1)} %copy-done, f32[1,2048]{1,0:T(1,128)S(1)} %bitcast.3), custom_call_target="tpu_custom_call" | custom-call | tf_op jit(solution)/shard_map/gather_sums/pallas_call | solution.py:230
  45.9 2.0 %copy.4 = f32[1,512,2048]{2,1,0:T(8,128)} copy(f32[1,512,2048]{2,1,0:T(8,128)S(1)} %bitcast.2) | data formatting | bytes 8388608
Async XLA Ops:
  0.0 1.0 %copy-start = (f32[256,512]{1,0:T(8,128)S(1)}, f32[256,512]{1,0:T(8,128)}, u32[]{:S(2)}) copy-start(f32[256,512]{1,0:T(8,128)} %returns_ref.1) | copy-start | bytes 1572868
  1.0 0.7 %copy-start.1 = (f32[2048]{0:T(1024)S(1)}, f32[2048]{0:T(1024)}, u32[]{:S(2)}) copy-start(f32[2048]{0:T(1024)} %param.3) | copy-start | bytes 24580

commit v3 on v2

--- a/solution.py
+++ b/solution.py
@@ -21,7 +21,7 @@
 
 
 def gather_kernel(
-    periods, tiles, returns_ref, rates_ref, out_ref, buf, left, cols, ssem, rsem
+    periods, tiles, returns_ref, rates_ref, out_ref, buf, left, ratio, cols, ssem, rsem
 ):
     seg_days, block = returns_ref.shape
     width = tiles // CORES
@@ -38,6 +38,7 @@
     x_dev, y_dev, p_dev = (sx, t), (s, yt), (s, pt)
     up_dev, down_dev = (s + width, t), (s - width, t)
     has_up, has_down = z < planes - 1, z > 0
+    up_half = 1 - c
 
     barrier = pltpu.get_barrier_semaphore()
     for dev in (x_dev, y_dev, p_dev):
@@ -63,7 +64,7 @@
     sent = []
 
     def copy(sp, tp, h, dev, sem):
-        part = buf.at[sp, tp, pl.ds(h * half, half)]
+        part = buf.at[sp, tp, pl.ds(pl.multiple_of(h * half, half), half)]
         return pltpu.make_async_remote_copy(
             part, part, sem, rsem.at[sp, tp, h], device_id=dev, device_id_type=MESH
         )
@@ -104,17 +105,21 @@
         def across(h):
             wait(x_gives, sb, t, h)
             if h == 0:
-                send(x_gives, sb, t, h, y_dev)
+                send(x_gives & (c == 0) if d else x_gives, sb, t, h, y_dev)
             send(x_gives, sb, t, h, p_dev)
             wait(exists, sa, yt, h)
             if h == 1:
-                send(x_takes, sa, yt, h, x_dev)
+                send(x_takes & (c == 1) if d else x_takes, sa, yt, h, x_dev)
+            if d == 0:
+                send((x == 1) & has_up & (up_half == h), sa, yt, h, x_dev)
             send(exists, sa, yt, h, p_dev)
 
         def corner():
-            for h in (0, 1):
-                wait(x_gives, sb, yt, h)
-                send(x_gives, sb, yt, h, p_dev)
+            wait(exists & has_up | x_gives, sb, yt, up_half)
+            send(exists & has_up, sb, yt, up_half, up_dev)
+            send(x_gives, sb, yt, up_half, p_dev)
+            wait(x_gives, sb, yt, 1 - up_half)
+            send(x_gives, sb, yt, 1 - up_half, p_dev)
 
         def transpose(sp):
             left[sp] = jnp.transpose(buf[sp, t])
@@ -179,21 +184,26 @@
 
     elapsed = ((s + 1) * seg_days).astype(F32)
 
-    def finish(first):
+    def weigh(first):
         u1, un = expm1_neg(-cols[...]), expm1_neg(-cols[...] * elapsed)
 
         def step(j, _):
             at = pl.ds(pl.multiple_of(first * block + j * 128, 128), 128)
             rates = rates_ref[:, at]
             v1, vn = expm1_neg(-rates), expm1_neg(-rates * elapsed)
-            out_ref[:, at] = out_ref[:, at] * ((u1 + v1 + u1 * v1) / (un + vn + un * vn))
+            ratio[:, at] = (u1 + v1 + u1 * v1) / (un + vn + un * vn)
             return 0
 
         lax.fori_loop(0, CORES * block // 128, step, 0)
+
+    def finish(first):
+        at = pl.ds(pl.multiple_of(first * block, block), CORES * block)
+        out_ref[:, at] = out_ref[:, at] * ratio[:, at]
 
     column[0](0)
     column[0](1)
     column_products[0]()
+    weigh(y * CORES)
     for d in range(planes):
         more = d + 1 < planes
         if more:
@@ -207,6 +217,8 @@
         if d:
             corner_products[d - 1]()
         across_products[d]()
+        if d == 1:
+            weigh((1 - y) * CORES)
         if more:
             column_products[d + 1]()
     finish(y * CORES)
@@ -235,8 +247,9 @@
         scratch_shapes=[
             pltpu.VMEM((periods, tiles, seg_days, block), jnp.bfloat16),
             pltpu.VMEM((periods, block, seg_days), jnp.bfloat16),
+            pltpu.VMEM((block, assets), F32),
             pltpu.VMEM((block, 128), F32),
-            pltpu.SemaphoreType.DMA((planes, 18)),
+            pltpu.SemaphoreType.DMA((planes, 20)),
             pltpu.SemaphoreType.DMA((periods, tiles, 2)),
         ],
         compiler_params=pltpu.CompilerParams(

time: 48.5 us -> 45.8 us (0.944)
  Pallas kernels: 44.1 us -> 41.3 us
    pallas_call x1, Pallas kernels: 44.1 us -> 41.3 us  [by_gather(): pl.pallas_call(functools.partial(gather_kernel, periods, tiles), out_shap...]
where the time goes in v3:
time: 45.8 us; the launch traced here: 45 us
  Pallas kernels  41.3 us (90%)
  local copies, waits for them, and re-layouts  3.75 us (8%)
    pallas_call x1, Pallas kernels, by_gather(): pl.pallas_call(functools.partial(gather_kernel, periods, tiles), out_shap...  41.3 us
    unnamed x5, local copies, waits for them, and re-layouts  3.75 us

profile of v3, /device:TPU:27, one launch (start us, length us, event | category | flops | bytes accessed | tf_op | source)
XLA Modules:
  0.0 45.0 jit_solution(7396650109833861318)
XLA Ops:
  0.0 0.0 copy-start
  0.0 1.0 %copy-done = f32[256,512]{1,0:T(8,128)S(1)} copy-done((f32[256,512]{1,0:T(8,128)S(1)}, f32[256,512]{1,0:T(8,128)}, u32[]{:S(2)}) %copy-start) | copy-done | bytes 524312
  1.0 0.0 copy-start.1
  1.0 0.7 %copy-done.1 = f32[2048]{0:T(1024)S(1)} copy-done((f32[2048]{0:T(1024)S(1)}, f32[2048]{0:T(1024)}, u32[]{:S(2)}) %copy-start.1) | copy-done | bytes 8216
  1.7 41.3 %gather_sums.1 = f32[512,2048]{1,0:T(8,128)S(1)} custom-call(f32[256,512]{1,0:T(8,128)S(1)} %copy-done, f32[1,2048]{1,0:T(1,128)S(1)} %bitcast.3), custom_call_target="tpu_custom_call" | custom-call | tf_op jit(solution)/shard_map/gather_sums/pallas_call | solution.py:242
  43.0 2.0 %copy.4 = f32[1,512,2048]{2,1,0:T(8,128)} copy(f32[1,512,2048]{2,1,0:T(8,128)S(1)} %bitcast.2) | data formatting | bytes 8388608
Async XLA Ops:
  0.0 1.0 %copy-start = (f32[256,512]{1,0:T(8,128)S(1)}, f32[256,512]{1,0:T(8,128)}, u32[]{:S(2)}) copy-start(f32[256,512]{1,0:T(8,128)} %returns_ref.1) | copy-start | bytes 1572868
  1.0 0.7 %copy-start.1 = (f32[2048]{0:T(1024)S(1)}, f32[2048]{0:T(1024)}, u32[]{:S(2)}) copy-start(f32[2048]{0:T(1024)} %param.3) | copy-start | bytes 24580

commit v4 on v3

--- a/solution.py
+++ b/solution.py
@@ -38,7 +38,7 @@
     x_dev, y_dev, p_dev = (sx, t), (s, yt), (s, pt)
     up_dev, down_dev = (s + width, t), (s - width, t)
     has_up, has_down = z < planes - 1, z > 0
-    up_half = 1 - c
+    up_half = 1
 
     barrier = pltpu.get_barrier_semaphore()
     for dev in (x_dev, y_dev, p_dev):
@@ -108,10 +108,10 @@
                 send(x_gives & (c == 0) if d else x_gives, sb, t, h, y_dev)
             send(x_gives, sb, t, h, p_dev)
             wait(exists, sa, yt, h)
-            if h == 1:
-                send(x_takes & (c == 1) if d else x_takes, sa, yt, h, x_dev)
-            if d == 0:
-                send((x == 1) & has_up & (up_half == h), sa, yt, h, x_dev)
+            if d == 0 and h == 1:
+                send(x_takes | has_up, sa, yt, h, x_dev)
+            if d and h == 0:
+                send(x_takes & (c == 1), sa, yt, h, x_dev)
             send(exists, sa, yt, h, p_dev)
 
         def corner():
@@ -216,13 +216,14 @@
         across[d](1)
         if d:
             corner_products[d - 1]()
+        if not more:
+            corner[d]()
         across_products[d]()
         if d == 1:
             weigh((1 - y) * CORES)
         if more:
             column_products[d + 1]()
     finish(y * CORES)
-    corner[-1]()
     corner_products[-1]()
     finish((1 - y) * CORES)
 

time: 45.8 us -> 44.2 us (0.965); the launches traced: 45 us -> 44 us
  Pallas kernels: 41.3 us -> 40.2 us
    pallas_call x1, Pallas kernels: 41.3 us -> 40.2 us  [by_gather(): pl.pallas_call(functools.partial(gather_kernel, periods, tiles), out_shap...]
where the time goes in v4:
time: 44.2 us; the launch traced here: 44 us
  Pallas kernels  40.2 us (91%)
  local copies, waits for them, and re-layouts  3.75 us (8%)
    pallas_call x1, Pallas kernels, by_gather(): pl.pallas_call(functools.partial(gather_kernel, periods, tiles), out_shap...  40.2 us
    unnamed x5, local copies, waits for them, and re-layouts  3.75 us

profile of v4, /device:TPU:27, one launch (start us, length us, event | category | flops | bytes accessed | tf_op | source)
XLA Modules:
  0.0 44.0 jit_solution(8457237817879383994)
XLA Ops:
  0.0 0.0 copy-start
  0.0 1.0 %copy-done = f32[256,512]{1,0:T(8,128)S(1)} copy-done((f32[256,512]{1,0:T(8,128)S(1)}, f32[256,512]{1,0:T(8,128)}, u32[]{:S(2)}) %copy-start) | copy-done | bytes 524312
  1.0 0.0 copy-start.1
  1.0 0.7 %copy-done.1 = f32[2048]{0:T(1024)S(1)} copy-done((f32[2048]{0:T(1024)S(1)}, f32[2048]{0:T(1024)}, u32[]{:S(2)}) %copy-start.1) | copy-done | bytes 8216
  1.7 40.2 %gather_sums.1 = f32[512,2048]{1,0:T(8,128)S(1)} custom-call(f32[256,512]{1,0:T(8,128)S(1)} %copy-done, f32[1,2048]{1,0:T(1,128)S(1)} %bitcast.3), custom_call_target="tpu_custom_call" | custom-call | tf_op jit(solution)/shard_map/gather_sums/pallas_call | solution.py:243
  42.0 2.0 %copy.4 = f32[1,512,2048]{2,1,0:T(8,128)} copy(f32[1,512,2048]{2,1,0:T(8,128)S(1)} %bitcast.2) | data formatting | bytes 8388608
Async XLA Ops:
  0.0 1.0 %copy-start = (f32[256,512]{1,0:T(8,128)S(1)}, f32[256,512]{1,0:T(8,128)}, u32[]{:S(2)}) copy-start(f32[256,512]{1,0:T(8,128)} %returns_ref.1) | copy-start | bytes 1572868
  1.0 0.7 %copy-start.1 = (f32[2048]{0:T(1024)S(1)}, f32[2048]{0:T(1024)}, u32[]{:S(2)}) copy-start(f32[2048]{0:T(1024)} %param.3) | copy-start | bytes 24580
